TPU v7x, 32 devices: a whole 2x2x4 slice. The times are simulated.
32 devices in a mesh: act: 4 (over y, x), virt: 8 (over z, core).
Axes of the slice: x: 2, y: 2, z: 4, core: 2. Of those that a mesh axis runs over, the one named last changes fastest.
Arguments:
- amplitudes: bfloat16 [400, 640, 640], P('act', 'virt'), may hold values from -6 to 6
- virtual_fock_block: bfloat16 [640, 640], replicated, may hold values from -1 to 3.1, as said below
- metric: bfloat16 [400, 400], replicated, may hold values from -3.5 to 3.5, as said below
- active_block: bfloat16 [400, 400], replicated, may hold values from -0.3125 to 0.3125
Outputs:
- residual_vec: bfloat16 [400, 640, 640], P('act', 'virt')
- rayleigh: float32 [], replicated
- res_norm: float32 [], replicated
Inputs may be any that keep to these rules, and one draw needn't show every extreme that they name: `virtual_fock_block`: symmetric. `metric`: symmetric positive definite.
All inputs are finite; a program needn't handle non-finite values.
Results may differ from a plain program's by a relative error of at most 0.0099.
Values may be sent and summed in bfloat16 or wider, within the bound.
A program may use at most 192 MiB of HBM per device.

v0:
```python
import functools

import jax
import jax.numpy as jnp
from jax import lax
from jax.experimental import pallas as pl
from jax.experimental.pallas import tpu as pltpu
from jax.sharding import PartitionSpec as P

MESH = pl.DeviceIdType.MESH
AHEAD = 4


def stage_kernel(first, peers, groups, pair_count, start, *refs):
    if first:
        (shift_ref, fock_ref, metric_ref, active_ref, image_ref, rows_ref,
         left_ref, back_ref, kept_ref, early_ref) = refs[:10]
        *scratch, early_sent, early_landed = refs[10:]
    else:
        fock_ref, metric_ref, kept_ref, image_ref, rows_ref, left_ref, back_ref = refs[:7]
        scratch = refs[7:]
    (held, made, row_held, row_made, sent, landed, back_sent, back_landed,
     row_sent, row_landed, row_back_sent, row_back_landed) = scratch
    group = lax.axis_index("act")
    me = lax.axis_index("virt")
    rounds, rows, width = held.shape[0], held.shape[2], held.shape[3]
    items = row_held.shape[0]
    per_step = -(-items // rounds)
    barrier = pltpu.get_barrier_semaphore()
    for step in range(1, peers):
        pl.semaphore_signal(
            barrier, inc=1, device_id=(group, lax.rem(me + step, peers)), device_id_type=MESH)
    for step in range(1, groups):
        pl.semaphore_signal(
            barrier, inc=1, device_id=(lax.rem(group + step, groups), me), device_id_type=MESH)
    pl.semaphore_wait(barrier, peers + groups - 2)

    whole_rounds = pair_count // peers
    spare = pair_count % peers
    stride = peers // spare if spare and peers % spare == 0 else 1

    def pair_of(r, owner):
        return r * peers + owner - (r // whole_rounds) * (owner - owner // stride)

    def owns(r, owner):
        return (r // whole_rounds) * peers * lax.rem(owner, stride) + pair_of(r, owner) < pair_count

    def slab(t):
        return image_ref.at[t, :, pl.ds(start, width)]

    def forward(r, peer):
        return pltpu.make_async_remote_copy(
            src_ref=slab(pair_of(r, peer)), dst_ref=held.at[r, me],
            send_sem=sent.at[r, peer], recv_sem=landed.at[r, me],
            device_id=(group, peer), device_id_type=MESH)

    def forward_own(r):
        return pltpu.make_async_copy(slab(pair_of(r, me)), held.at[r, me], landed.at[r, me])

    def arrival(r, peer):
        return pltpu.make_async_remote_copy(
            src_ref=made.at[r, peer], dst_ref=held.at[r, peer],
            send_sem=sent.at[r, peer], recv_sem=landed.at[r, peer],
            device_id=(group, peer), device_id_type=MESH)

    def backward(r, peer):
        return pltpu.make_async_remote_copy(
            src_ref=made.at[r, peer], dst_ref=left_ref.at[pair_of(r, me)],
            send_sem=back_sent.at[r, peer], recv_sem=back_landed.at[r, me],
            device_id=(group, peer), device_id_type=MESH)

    def backward_own(r):
        return pltpu.make_async_copy(made.at[r, me], left_ref.at[pair_of(r, me)], back_landed.at[r, me])

    def back_arrival(r, peer):
        return pltpu.make_async_remote_copy(
            src_ref=made.at[r, peer], dst_ref=left_ref.at[pair_of(r, peer)],
            send_sem=back_sent.at[r, peer], recv_sem=back_landed.at[r, peer],
            device_id=(group, peer), device_id_type=MESH)

    def row_forward(i, peer):
        return pltpu.make_async_remote_copy(
            src_ref=rows_ref.at[peer * items + i], dst_ref=row_held.at[i, group],
            send_sem=row_sent.at[i, peer], recv_sem=row_landed.at[i, group],
            device_id=(peer, me), device_id_type=MESH)

    def row_forward_own(i):
        return pltpu.make_async_copy(
            rows_ref.at[group * items + i], row_held.at[i, group], row_landed.at[i, group])

    def row_arrival(i, peer):
        return pltpu.make_async_remote_copy(
            src_ref=rows_ref.at[peer * items + i], dst_ref=row_held.at[i, peer],
            send_sem=row_sent.at[i, peer], recv_sem=row_landed.at[i, peer],
            device_id=(peer, me), device_id_type=MESH)

    def row_backward(i, peer):
        return pltpu.make_async_remote_copy(
            src_ref=row_made.at[i, peer], dst_ref=back_ref.at[group * items + i],
            send_sem=row_back_sent.at[i, peer], recv_sem=row_back_landed.at[i, group],
            device_id=(peer, me), device_id_type=MESH)

    def row_backward_own(i):
        return pltpu.make_async_copy(
            row_made.at[i, group], back_ref.at[group * items + i], row_back_landed.at[i, group])

    def row_back_arrival(i, peer):
        return pltpu.make_async_remote_copy(
            src_ref=row_made.at[i, peer], dst_ref=back_ref.at[peer * items + i],
            send_sem=row_back_sent.at[i, peer], recv_sem=row_back_landed.at[i, peer],
            device_id=(peer, me), device_id_type=MESH)

    if first:
        early_width = early_ref.shape[2]
        early_columns = pl.ds(kept_ref.shape[3] - early_width, early_width)

        def early(i, peer):
            return pltpu.make_async_remote_copy(
                src_ref=kept_ref.at[i, peer, :, early_columns], dst_ref=early_ref.at[group * items + i],
                send_sem=early_sent.at[i, peer], recv_sem=early_landed.at[i, group],
                device_id=(peer, me), device_id_type=MESH)

        def early_own(i):
            return pltpu.make_async_copy(
                kept_ref.at[i, group, :, early_columns], early_ref.at[group * items + i],
                early_landed.at[i, group])

        def early_arrival(i, peer):
            return pltpu.make_async_remote_copy(
                src_ref=kept_ref.at[i, peer, :, early_columns], dst_ref=early_ref.at[peer * items + i],
                send_sem=early_sent.at[i, peer], recv_sem=early_landed.at[i, peer],
                device_id=(peer, me), device_id_type=MESH)

    def launch(r):
        for step in range(peers):
            peer = lax.rem(me + step, peers)

            @pl.when(owns(r, peer))
            def _(step=step, peer=peer):
                if step == 0:
                    forward_own(r).start()
                else:
                    forward(r, peer).start()

        def launch_row(i, carry):
            row_forward_own(i).start()
            for step in range(1, groups):
                row_forward(i, lax.rem(group + step, groups)).start()
            return carry

        lax.fori_loop(jnp.minimum(r * per_step, items), jnp.minimum((r + 1) * per_step, items), launch_row, 0)

    def ahead(r, carry):
        launch(r)
        return carry

    lax.fori_loop(0, min(AHEAD, rounds), ahead, 0)

    def mix(matrix_ref, i):
        total = jnp.dot(matrix_ref[0], row_held[i, 0], preferred_element_type=jnp.float32)
        for q in range(1, groups):
            total += jnp.dot(matrix_ref[q], row_held[i, q], preferred_element_type=jnp.float32)
        return total.reshape(groups, -1, total.shape[1])[:, :row_held.shape[2]]

    def mix_row(i, carry):
        row_forward_own(i).wait()
        for step in range(1, groups):
            row_arrival(i, lax.rem(group + step, groups)).wait_recv()
        weighted = mix(metric_ref, i)
        if first:
            half = weighted.astype(jnp.bfloat16)
            row_made[i] = half
            active = mix(active_ref, i) - shift_ref[0] * (weighted - half.astype(jnp.float32))
            kept_ref[i] = active.astype(jnp.bfloat16)
            early_own(i).start()
            for step in range(1, groups):
                early(i, lax.rem(group + step, groups)).start()
        else:
            wide, part = row_held.shape[3], row_made.shape[3]
            kept = kept_ref[i, :, :, :wide].astype(jnp.float32)
            row_made[i, :, :, :wide] = (kept + weighted).astype(jnp.bfloat16)
            if part > wide:
                row_made[i, :, :, wide:] = kept_ref[i, :, :, wide:part]
        row_backward_own(i).start()
        for step in range(1, groups):
            row_backward(i, lax.rem(group + step, groups)).start()
        return carry

    def body(r, carry):
        @pl.when(r + AHEAD < rounds)
        def _():
            launch(r + AHEAD)

        lax.fori_loop(jnp.minimum(r * per_step, items), jnp.minimum((r + 1) * per_step, items), mix_row, 0)

        @pl.when(owns(r, me))
        def _():
            forward_own(r).wait()
            for step in range(1, peers):
                arrival(r, lax.rem(me + step, peers)).wait_recv()
            block = held[r].reshape(peers * rows, width)
            product = jnp.dot(fock_ref[...], block, preferred_element_type=jnp.float32)
            made[r] = product.astype(jnp.bfloat16).reshape(peers, rows, width)
            backward_own(r).start()
            for step in range(1, peers):
                backward(r, lax.rem(me + step, peers)).start()

        return carry

    lax.fori_loop(0, rounds, body, 0)

    def drain(r, carry):
        mine = owns(r, me)

        @pl.when(mine)
        def _():
            backward_own(r).wait()

        for step in range(1, peers):
            peer = lax.rem(me + step, peers)

            @pl.when(owns(r, peer))
            def _(peer=peer):
                forward(r, peer).wait_send()
                back_arrival(r, peer).wait_recv()

            @pl.when(mine)
            def _(peer=peer):
                backward(r, peer).wait_send()

        return carry

    lax.fori_loop(0, rounds, drain, 0)

    def drain_row(i, carry):
        row_backward_own(i).wait()
        for step in range(1, groups):
            peer = lax.rem(group + step, groups)
            row_forward(i, peer).wait_send()
            row_back_arrival(i, peer).wait_recv()
            row_backward(i, peer).wait_send()
            if first:
                early_arrival(i, peer).wait_recv()
                early(i, peer).wait_send()
        if first:
            early_own(i).wait()
        return carry

    lax.fori_loop(0, items, drain_row, 0)


def stage(first, peers, groups, pairs, start, width, tail, smalls, kept, image, turned):
    fock = smalls[1] if first else smalls[0]
    padded = image.shape[1]
    count, tall, row_width = turned.shape
    items = count // groups
    rounds = -(-pairs // peers)
    full = image.shape[2]
    whole = pl.BlockSpec(memory_space=pltpu.VMEM)
    anywhere = pl.BlockSpec(memory_space=pl.ANY)
    kept_rows = (items, groups, tall, full)
    made_width = full if first else full - tail
    out_shape = [
        jax.ShapeDtypeStruct((pairs, padded, width), jnp.bfloat16),
        jax.ShapeDtypeStruct((count, tall, made_width), jnp.bfloat16),
    ]
    out_specs = [anywhere, anywhere]
    if first:
        in_specs = [pl.BlockSpec(memory_space=pltpu.SMEM)] + [whole] * 3
        out_shape.append(jax.ShapeDtypeStruct(kept_rows, jnp.bfloat16))
        out_shape.append(jax.ShapeDtypeStruct((count, tall, tail), jnp.bfloat16))
        out_specs += [whole, anywhere]
        operands = smalls
    else:
        in_specs = [whole] * 3
        operands = (*smalls, kept)
    dma = pltpu.SemaphoreType.DMA
    return pl.pallas_call(
        functools.partial(stage_kernel, first, peers, groups, pairs, start),
        out_shape=out_shape,
        in_specs=in_specs + [anywhere] * 2,
        out_specs=out_specs,
        scratch_shapes=[
            pltpu.VMEM((rounds, peers, padded, width), jnp.bfloat16),
            pltpu.VMEM((rounds, peers, padded, width), jnp.bfloat16),
            pltpu.VMEM((items, groups, tall, row_width), jnp.bfloat16),
            pltpu.VMEM((items, groups, tall, made_width), jnp.bfloat16),
            dma((rounds, peers)), dma((rounds, peers)), dma((rounds, peers)), dma((rounds, peers)),
            dma((items, groups)), dma((items, groups)), dma((items, groups)), dma((items, groups)),
        ] + [dma((items, groups))] * (2 if first else 0),
        compiler_params=pltpu.CompilerParams(
            collective_id=1 if first else 2, has_side_effects=True, vmem_limit_bytes=60 * 2**20),
        cost_estimate=pl.CostEstimate(
            flops=2 * pairs * fock.size * width, bytes_accessed=400 * 2**20, transcendentals=0),
    )(*operands, image, turned)


def finish_kernel(groups, peers, fock_ref, trial_ref, image_ref, left_ref, rest_ref, early_ref, out_ref, stats_ref,
                  trial, image, left, rest, sigma, part, slots, loaded, stored, sent, landed):
    group, me = lax.axis_index("act"), lax.axis_index("virt")
    count = groups * peers
    mine = group * peers + me
    barrier = pltpu.get_barrier_semaphore()
    chunks = loaded.shape[1]
    depth = trial.shape[0] // chunks
    rows, width = trial.shape[1], trial.shape[2]
    tail = left.shape[2]
    cut = width - tail

    def span(c):
        return pl.ds(c * depth, depth)

    def load(c, which):
        source, target = ((trial_ref, trial), (image_ref, image), (left_ref, left))[which]
        return pltpu.make_async_copy(source.at[span(c)], target.at[span(c)], loaded.at[which, c])

    def load_rest(c):
        head = rest_ref.shape[2]
        return (
            pltpu.make_async_copy(
                rest_ref.at[span(c)], rest.at[span(c), :, pl.ds(0, head)], loaded.at[3, c]),
            pltpu.make_async_copy(
                early_ref.at[span(c)], rest.at[span(c), :, pl.ds(head, width - head)], loaded.at[4, c]))

    def load_all(c, carry):
        for which in range(3):
            load(c, which).start()
        for copy in load_rest(c):
            copy.start()
        return carry

    lax.fori_loop(0, chunks, load_all, 0)

    def target(step):
        other = lax.rem(mine + step, count)
        return other, (other // peers, lax.rem(other, peers))

    def greet(step, carry):
        pl.semaphore_signal(barrier, inc=1, device_id=target(step)[1], device_id_type=MESH)
        return carry

    lax.fori_loop(1, count, greet, 0)

    def product(c, carry):
        numer, denom = carry
        for which in range(3):
            load(c, which).wait()
        for copy in load_rest(c):
            copy.wait()
        own = image[span(c)].reshape(depth * rows, width)
        total = jnp.dot(own, fock_ref[...], preferred_element_type=jnp.float32)
        total += rest[span(c)].reshape(depth * rows, width).astype(jnp.float32)
        last = total[:, cut:] + left[span(c)].reshape(depth * rows, tail).astype(jnp.float32)
        total = jnp.concatenate([total[:, :cut], last], axis=1)
        sigma[span(c)] = total.reshape(depth, rows, width)
        wide = trial[span(c)].reshape(depth * rows, width).astype(jnp.float32)
        numer += jnp.sum(wide * total, axis=0, keepdims=True)
        denom += jnp.sum(wide * own.astype(jnp.float32), axis=0, keepdims=True)
        return numer, denom

    zero = jnp.zeros((1, width), jnp.float32)
    numer, denom = lax.fori_loop(0, chunks, product, (zero, zero))
    pl.semaphore_wait(barrier, count - 1)

    def sum_all(phase, value):
        part[phase] = value

        def copy(step, slot):
            other, place = target(step)
            return pltpu.make_async_remote_copy(
                src_ref=part.at[phase], dst_ref=slots.at[phase, slot],
                send_sem=sent.at[phase, other], recv_sem=landed.at[phase, slot],
                device_id=place, device_id_type=MESH)

        def send(step, carry):
            copy(step, mine).start()
            return carry

        lax.fori_loop(1, count, send, 0)
        slots[phase, mine] = value

        def receive(step, carry):
            copy(step, target(step)[0]).wait_recv()
            return carry

        lax.fori_loop(1, count, receive, 0)

        def finish(step, carry):
            copy(step, mine).wait_send()
            return carry

        lax.fori_loop(1, count, finish, 0)
        return jnp.sum(slots[phase], axis=0)

    row = lax.broadcasted_iota(jnp.int32, (8, 128), 0)
    numer_one = jnp.sum(numer, axis=1, keepdims=True)
    denom_one = jnp.sum(denom, axis=1, keepdims=True)
    sums = sum_all(0, jnp.where(row == 0, numer_one, denom_one))
    denominator = sums[1:2, 0:1]
    rayleigh = sums[0:1, 0:1] / denominator

    def store(c):
        return pltpu.make_async_copy(rest.at[span(c)], out_ref.at[span(c)], stored.at[c])

    def residual(c, squares):
        own = image[span(c)].reshape(depth * rows, width).astype(jnp.float32)
        resid = sigma[span(c)].reshape(depth * rows, width) - rayleigh * own
        rest[span(c)] = resid.astype(jnp.bfloat16).reshape(depth, rows, width)
        store(c).start()
        return squares + jnp.sum(resid * resid, axis=0, keepdims=True)

    squares = lax.fori_loop(0, chunks, residual, zero)
    square_one = jnp.sum(squares, axis=1, keepdims=True)
    norms = sum_all(1, jnp.broadcast_to(square_one, (8, 128)))
    stats_ref[...] = jnp.where(row == 0, rayleigh, norms / denominator)

    def drain(c, carry):
        store(c).wait()
        return carry

    lax.fori_loop(0, chunks, drain, 0)


def finish(groups, peers, fock, trial, image, left, rest, early):
    pairs, rows, width = trial.shape
    depth = next(d for d in (5, 4, 2, 1) if pairs % d == 0)
    chunks = pairs // depth
    whole = pl.BlockSpec(memory_space=pltpu.VMEM)
    anywhere = pl.BlockSpec(memory_space=pl.ANY)
    dma = pltpu.SemaphoreType.DMA
    count = groups * peers
    return pl.pallas_call(
        functools.partial(finish_kernel, groups, peers),
        out_shape=[
            jax.ShapeDtypeStruct((pairs, rows, width), jnp.bfloat16),
            jax.ShapeDtypeStruct((8, 128), jnp.float32),
        ],
        in_specs=[whole] + [anywhere] * 5,
        out_specs=[anywhere, whole],
        scratch_shapes=[
            pltpu.VMEM((pairs, rows, width), jnp.bfloat16),
            pltpu.VMEM((pairs, rows, width), jnp.bfloat16),
            pltpu.VMEM((pairs, rows, left.shape[2]), jnp.bfloat16),
            pltpu.VMEM((pairs, rows, width), jnp.bfloat16),
            pltpu.VMEM((pairs, rows, width), jnp.float32),
            pltpu.VMEM((2, 8, 128), jnp.float32),
            pltpu.VMEM((2, count, 8, 128), jnp.float32),
            dma((5, chunks)), dma((chunks,)), dma((2, count)), dma((2, count)),
        ],
        compiler_params=pltpu.CompilerParams(
            collective_id=3, has_side_effects=True, vmem_limit_bytes=63 * 2**20),
    )(fock, trial, image, left, rest, early)


def local(amplitudes, virtual_fock_block, metric, active_block):
    pairs, rows, width = amplitudes.shape
    peers, groups = lax.axis_size("virt"), lax.axis_size("act")
    fock = virtual_fock_block
    padded = -(-rows // 16) * 16
    room = -pairs % 8
    cut = (3 * width // 5) // 128 * 128

    def widen(array):
        if padded == rows:
            return array
        return jnp.pad(array, ((0, 0), (0, padded - rows), (0, 0)))

    def turn(array):
        return jnp.transpose(array, (1, 0, 2))

    def turn_back(array):
        return jnp.transpose(array, (1, 0, 2))

    def pair_matrix(array):
        spread = jnp.pad(array.reshape(groups, pairs, groups, pairs), ((0, 0), (0, room), (0, 0), (0, 0)))
        return jnp.transpose(spread, (2, 0, 1, 3)).reshape(groups, groups * (pairs + room), pairs)

    spread = fock
    if padded != rows:
        gap = padded - rows
        spread = jnp.pad(
            fock.reshape(peers, rows, peers, rows), ((0, 0), (0, gap), (0, 0), (0, gap))
        ).reshape(peers * padded, peers * padded)
    metric_parts, active_parts = pair_matrix(metric), pair_matrix(active_block)
    at = lax.broadcasted_iota(jnp.int32, fock.shape, 0)
    across = lax.broadcasted_iota(jnp.int32, fock.shape, 1)
    shift = (2.0 / width) * jnp.sum(jnp.where(at == across, fock.astype(jnp.float32), 0.0))
    trial = widen(amplitudes)
    tail = min(128, width - cut)
    applied, weighted_turned, kept, early_turned = stage(
        True, peers, groups, pairs, 0, cut, tail, (shift.reshape(1), spread, metric_parts, active_parts),
        None, trial, turn(amplitudes))
    weighted = widen(turn_back(weighted_turned))
    left, rest_turned = stage(
        False, peers, groups, pairs, cut, width - cut, tail, (spread, metric_parts),
        kept, weighted, turn(applied[:, :rows]))
    rest = widen(turn_back(rest_turned))
    early = widen(turn_back(early_turned))
    resid, stats = finish(groups, peers, fock, trial, weighted, left, rest, early)
    return resid[:, :rows], stats[0, 0], stats[1, 0]


def solution(mesh):
    placed = (P("act", "virt", None), P(), P(), P())
    return jax.shard_map(
        local,
        mesh=mesh,
        in_specs=placed,
        out_specs=(P("act", "virt", None), P(), P()),
        check_vma=False,
    )
```

profile of v0, /device:TPU:0, one launch (start us, length us, event | category | flops | bytes accessed | tf_op | source)
XLA Modules:
  0.0 571.2 jit_solution(9776829869237930080)
XLA Ops:
  0.6 1.8 select_reduce_fusion
  3.1 1.3 reshape.22
  4.4 0.1 copy.7
  4.5 0.9 pad.7
  5.3 1.3 reshape.24
  6.6 0.1 copy.8
  6.7 0.8 pad.8
  7.5 11.5 %copy.19 = bf16[100,80,640]{2,0,1:T(8,128)(2,1)} copy(bf16[100,80,640]{2,1,0:T(8,128)(2,1)} %trial_ref.1) | data formatting | bytes 20480000 | tf_op args[0]
  19.0 282.8 %shard_map.67 = (bf16[100,80,384]{2,1,0:T(8,128)(2,1)}, bf16[80,100,640]{2,1,0:T(8,128)(2,1)}, bf16[20,4,100,640]{3,2,1,0:T(8,128)(2,1)}, bf16[80,100,128]{2,1,0:T(8,128)(2,1)}) custom-call(f32[1]{0:T(128)} %bitcast.refs_0_, bf16[640,640]{1,0:T(8,128)(2,1)} %fock_ref.1, bf16[4,416,100]{2,1,0:T(8,128)(2,1)} %bitcast.30, bf16[4,416,100]{2,1,0:T(8,128)(2,1)} %bitcast.32, ...), custom_call_target="tpu_custom_call" | custom-call | flops 31457280000 | bytes 419430400 | tf_op jit(solution)/shard_map/pallas_call | solution.py:278
  301.8 0.0 copy-start
  301.8 9.5 %copy.20 = bf16[80,100,640]{2,0,1:T(8,128)(2,1)} copy(bf16[80,100,640]{2,1,0:T(8,128)(2,1)} %get-tuple-element.11) | data formatting | bytes 20480000 | tf_op jit(solution)/shard_map/pallas_call | solution.py:278
  311.3 0.0 copy-done
  311.3 1.6 copy.23
  312.9 6.8 %copy.22 = bf16[100,80,384]{2,0,1:T(8,128)(2,1)} copy(bf16[100,80,384]{2,1,0:T(8,128)(2,1)} %get-tuple-element.13) | data formatting | bytes 12288000 | tf_op jit(solution)/shard_map/pallas_call | solution.py:278
  319.7 191.8 %shard_map.68 = (bf16[100,80,256]{2,1,0:T(8,128)(2,1)}, bf16[80,100,512]{2,1,0:T(8,128)(2,1)}) custom-call(bf16[640,640]{1,0:T(8,128)(2,1)} %fock_ref.1, bf16[4,416,100]{2,1,0:T(8,128)(2,1)} %bitcast.31, bf16[20,4,100,640]{3,2,1,0:T(8,128)(2,1)} %get-tuple-element.12.refs_2_, bf16[100,80,640]{2,1,0:T(8,128)(2,1)} %bitcast.24, bf16[80,100,384]{2,1,0:T(8,128)(2,1)} %bitcast.29), custom_call_target="tpu_custom_call" | custom-call | flops 20971520000 | bytes 419430400 | tf_op jit(solution)/shard_map/pallas_call | solution.py:278
  511.5 9.6 %copy.21 = bf16[80,100,512]{2,0,1:T(8,128)(2,1)} copy(bf16[80,100,512]{2,1,0:T(8,128)(2,1)} %get-tuple-element.15) | data formatting | bytes 16384000 | tf_op jit(solution)/shard_map/pallas_call | solution.py:278
  521.1 40.0 %shard_map.69 = (bf16[100,80,640]{2,1,0:T(8,128)(2,1)}, f32[8,128]{1,0:T(8,128)}) custom-call(bf16[640,640]{1,0:T(8,128)(2,1)} %fock_ref.1, bf16[100,80,640]{2,1,0:T(8,128)(2,1)} %trial_ref.1, bf16[100,80,640]{2,1,0:T(8,128)(2,1)} %bitcast.25, bf16[100,80,256]{2,1,0:T(8,128)(2,1)} %get-tuple-element.14.left_ref, bf16[100,80,512]{2,1,0:T(8,128)(2,1)} %bitcast.26, ...), custom_call_target="tpu_custom_call" | custom-call | tf_op jit(solution)/shard_map/pallas_call | solution.py:432
  561.2 1.3 fusion
  562.5 8.8 %copy.25 = bf16[100,80,640]{2,1,0:T(8,128)(2,1)} copy(bf16[100,80,640]{2,1,0:T(8,128)(2,1)} %get-tuple-element.24) | data formatting | bytes 20480000
Async XLA Ops:
  301.8 9.5 %copy-start = (bf16[80,100,128]{2,1,0:T(8,128)(2,1)S(1)}, bf16[80,100,128]{2,1,0:T(8,128)(2,1)}, u32[]{:S(2)}) copy-start(bf16[80,100,128]{2,1,0:T(8,128)(2,1)} %get-tuple-element.16) | copy-start | bytes 6144004
where the time goes:
time: 572 us; the launch traced here: 571 us
  Pallas kernels  515 us (90%)
  local copies, waits for them, and re-layouts  53.4 us (9%)
    pallas_call x2, Pallas kernels, stage(): pl.pallas_call(functools.partial(stage_kernel, first, peers, groups, pair...  475 us
    pallas_call x1, Pallas kernels, finish(): pl.pallas_call(functools.partial(finish_kernel, groups, peers), out_shape...  40 us
    pallas_call x4, local copies, waits for them, and re-layouts, stage(): pl.pallas_call(functools.partial(stage_kernel, first, peers, groups, pair...  27.4 us
    unnamed x4, local copies, waits for them, and re-layouts  20.3 us

commit v1 on v0

v1 whole, which is shorter than its diff:
```python
import functools

import jax
import jax.numpy as jnp
from jax import lax
from jax.experimental import pallas as pl
from jax.experimental.pallas import tpu as pltpu
from jax.sharding import PartitionSpec as P

MESH = pl.DeviceIdType.MESH
AHEAD = 4


HIGH = 16
SLOTS = 8
WINDOW = 8


def main_kernel(groups, peers, rows, cut, shift_ref, fock_ref, metric_ref, active_ref, trial_ref,
                trial_rows, image_rows, image_ref, front_ref, front_rows, left_ref, rest_rows, rest_ref,
                held_a, held_b, made_a, made_b, late_held, soon_held, front_held, late_image, soon_image,
                late_kept, soon_kept, rest_made, flat, turned, sems_a, sems_b, act_sems, loaded, stored):
    group, me = lax.axis_index("act"), lax.axis_index("virt")
    pairs, padded, width = trial_ref.shape
    rounds = held_a.shape[0]
    items = rows // groups
    chunks = padded // HIGH
    per_chunk = HIGH // groups
    soon, late = pl.ds(0, cut), pl.ds(cut, width - cut)

    barrier = pltpu.get_barrier_semaphore()
    for step in range(1, peers):
        pl.semaphore_signal(
            barrier, inc=1, device_id=(group, lax.rem(me + step, peers)), device_id_type=MESH)
    for step in range(1, groups):
        pl.semaphore_signal(
            barrier, inc=1, device_id=(lax.rem(group + step, groups), me), device_id_type=MESH)

    whole_rounds = pairs // peers
    spare = pairs % peers
    stride = peers // spare if spare and peers % spare == 0 else 1

    def pair_of(r, owner):
        return r * peers + owner - (r // whole_rounds) * (owner - owner // stride)

    def owns(r, owner):
        return (r // whole_rounds) * peers * lax.rem(owner, stride) + pair_of(r, owner) < pairs

    class Fock:
        def __init__(self, source, columns, held, made, target, sems):
            self.source, self.columns, self.held, self.made = source, columns, held, made
            self.target, self.sems, self.ring = target, sems, made.shape[0]

        def slab(self, t):
            return self.source.at[t, :, self.columns]

        def forward(self, r, peer):
            return pltpu.make_async_remote_copy(
                src_ref=self.slab(pair_of(r, peer)), dst_ref=self.held.at[r, me],
                send_sem=self.sems.at[0, r, peer], recv_sem=self.sems.at[1, r, me],
                device_id=(group, peer), device_id_type=MESH)

        def forward_own(self, r):
            return pltpu.make_async_copy(
                self.slab(pair_of(r, me)), self.held.at[r, me], self.sems.at[1, r, me])

        def arrival(self, r, peer):
            return pltpu.make_async_remote_copy(
                src_ref=self.held.at[r, me], dst_ref=self.held.at[r, peer],
                send_sem=self.sems.at[0, r, peer], recv_sem=self.sems.at[1, r, peer],
                device_id=(group, peer), device_id_type=MESH)

        def backward(self, r, peer):
            return pltpu.make_async_remote_copy(
                src_ref=self.made.at[lax.rem(r, self.ring), peer], dst_ref=self.target.at[pair_of(r, me)],
                send_sem=self.sems.at[2, r, peer], recv_sem=self.sems.at[3, r, me],
                device_id=(group, peer), device_id_type=MESH)

        def backward_own(self, r):
            return pltpu.make_async_copy(
                self.made.at[lax.rem(r, self.ring), me], self.target.at[pair_of(r, me)], self.sems.at[3, r, me])

        def back_arrival(self, r, peer):
            return pltpu.make_async_remote_copy(
                src_ref=self.made.at[0, peer], dst_ref=self.target.at[pair_of(r, peer)],
                send_sem=self.sems.at[2, r, peer], recv_sem=self.sems.at[3, r, peer],
                device_id=(group, peer), device_id_type=MESH)

        def launch(self, r):
            for step in range(peers):
                peer = lax.rem(me + step, peers)

                @pl.when(owns(r, peer))
                def _(step=step, peer=peer):
                    if step == 0:
                        self.forward_own(r).start()
                    else:
                        self.forward(r, peer).start()

        def launch_first(self):
            def ahead(r, carry):
                self.launch(r)
                return carry

            lax.fori_loop(0, min(AHEAD, rounds), ahead, 0)

        def launch_next(self, r):
            @pl.when(r + AHEAD < rounds)
            def _():
                self.launch(r + AHEAD)

        def sent_back(self, r):
            for step in range(1, peers):
                self.backward(r, lax.rem(me + step, peers)).wait_send()

        def apply(self, r):
            @pl.when(r >= 1)
            def _():
                self.backward_own(r - 1).wait()

            @pl.when(owns(r, me))
            def _():
                self.forward_own(r).wait()
                for step in range(1, peers):
                    self.arrival(r, lax.rem(me + step, peers)).wait_recv()

                @pl.when(r >= self.ring)
                def _():
                    self.sent_back(r - self.ring)

                block = self.held[r].reshape(peers * padded, self.held.shape[3])
                product = jnp.dot(fock_ref[...], block, preferred_element_type=jnp.float32)
                self.made[lax.rem(r, self.ring)] = product.astype(jnp.bfloat16).reshape(
                    peers, padded, self.held.shape[3])
                self.backward_own(r).start()
                for step in range(1, peers):
                    self.backward(r, lax.rem(me + step, peers)).start()

        def settle(self):
            @pl.when(owns(rounds - 1, me))
            def _():
                self.backward_own(rounds - 1).wait()

            def landed(r, carry):
                for step in range(1, peers):
                    peer = lax.rem(me + step, peers)

                    @pl.when(owns(r, peer))
                    def _(peer=peer):
                        self.back_arrival(r, peer).wait_recv()

                return carry

            lax.fori_loop(0, rounds, landed, 0)

        def drain(self):
            def done(r, carry):
                for step in range(1, peers):
                    peer = lax.rem(me + step, peers)

                    @pl.when(owns(r, peer))
                    def _(peer=peer):
                        self.forward(r, peer).wait_send()

                return carry

            lax.fori_loop(0, rounds, done, 0)

            def back_done(r, carry):
                kept = (r + self.ring < rounds - 1) | ((r + self.ring == rounds - 1) & owns(rounds - 1, me))

                @pl.when(owns(r, me) & jnp.logical_not(kept))
                def _():
                    self.sent_back(r)

                return carry

            lax.fori_loop(0, rounds, back_done, 0)

    class Swap:
        def __init__(self, kind, source, target):
            self.kind, self.source, self.target = kind, source, target

        def send(self, i, peer):
            return pltpu.make_async_remote_copy(
                src_ref=self.source(i, peer), dst_ref=self.target(i, group),
                send_sem=act_sems.at[self.kind, 0, i, peer], recv_sem=act_sems.at[self.kind, 1, i, group],
                device_id=(peer, me), device_id_type=MESH)

        def own(self, i):
            return pltpu.make_async_copy(
                self.source(i, group), self.target(i, group), act_sems.at[self.kind, 1, i, group])

        def arrival(self, i, peer):
            return pltpu.make_async_remote_copy(
                src_ref=self.source(i, peer), dst_ref=self.target(i, peer),
                send_sem=act_sems.at[self.kind, 0, i, peer], recv_sem=act_sems.at[self.kind, 1, i, peer],
                device_id=(peer, me), device_id_type=MESH)

        def start(self, i):
            self.own(i).start()
            for step in range(1, groups):
                self.send(i, lax.rem(group + step, groups)).start()

        def wait_remote(self, i):
            for step in range(1, groups):
                self.arrival(i, lax.rem(group + step, groups)).wait_recv()

        def wait(self, i):
            self.own(i).wait()
            self.wait_remote(i)

        def sent(self, i):
            for step in range(1, groups):
                self.send(i, lax.rem(group + step, groups)).wait_send()

        def drain(self, first):
            def done(i, carry):
                self.sent(i)
                return carry

            lax.fori_loop(first, items, done, 0)

    def row(i, owner):
        return i * groups + owner

    def slot(i):
        return lax.rem(i, SLOTS)

    front = Fock(trial_ref, soon, held_a, made_a, front_ref, sems_a)
    back = Fock(image_ref, late, held_b, made_b, left_ref, sems_b)
    late_in = Swap(0, lambda i, p: trial_rows.at[row(i, p), :, late], lambda i, p: late_held.at[i, p])
    soon_in = Swap(1, lambda i, p: trial_rows.at[row(i, p), :, soon], lambda i, p: soon_held.at[i, p])
    late_out = Swap(2, lambda i, p: late_image.at[slot(i), p], lambda i, p: image_rows.at[row(i, p), :, late])
    soon_out = Swap(3, lambda i, p: soon_image.at[slot(i), p], lambda i, p: image_rows.at[row(i, p), :, soon])
    kept_out = Swap(4, lambda i, p: late_kept.at[i, p], lambda i, p: rest_rows.at[row(i, p), :, late])
    front_in = Swap(5, lambda i, p: front_rows.at[row(i, p)], lambda i, p: front_held.at[i, p])
    rest_out = Swap(6, lambda i, p: rest_made.at[slot(i), p], lambda i, p: rest_rows.at[row(i, p), :, soon])

    def run(low, high, work):
        def one(i, carry):
            work(i)
            return carry

        lax.fori_loop(low, high, one, 0)

    def strip(c):
        return pl.ds(pl.multiple_of(c * HIGH, HIGH), HIGH)

    def blocks(extent, work):
        def one(j, carry):
            work(pl.ds(pl.multiple_of(j * 128, 128), 128))
            return carry

        lax.fori_loop(0, extent // 128, one, 0)

    def to_rows(at, extent):
        def work(columns):
            turned[at, :, :, columns] = jnp.transpose(flat[at, :, :, columns], (1, 0, 2))

        blocks(extent, work)

    def to_flat(c, at, extent):
        def work(columns):
            block = jnp.transpose(turned[at, :, :, columns], (1, 0, 2))
            if padded != rows:
                place = c * HIGH + lax.broadcasted_iota(jnp.int32, block.shape, 1)
                block = jnp.where(place < rows, block, jnp.zeros_like(block))
            flat[at, :, :, columns] = block

        blocks(extent, work)

    def turn_back(c, source, target, columns, extent):
        load = pltpu.make_async_copy(
            source.at[strip(c), :, columns], turned.at[0, :, :, pl.ds(0, extent)], loaded.at[0])
        load.start()
        load.wait()
        to_flat(c, 0, extent)
        store = pltpu.make_async_copy(
            flat.at[0, :, :, pl.ds(0, extent)], target.at[:, strip(c), columns], stored.at[0])
        store.start()
        store.wait()

    def arrived(swap, c, work):
        run(c * per_chunk, jnp.minimum((c + 1) * per_chunk, items), work)

    def image_late(c):
        arrived(late_out, c, late_out.wait_remote)
        turn_back(c, image_rows, image_ref, late, width - cut)

    def image_soon(c):
        arrived(soon_out, c, soon_out.wait_remote)
        turn_back(c, image_rows, image_ref, soon, cut)

    def rest_late(c):
        arrived(kept_out, c, kept_out.wait)
        turn_back(c, rest_rows, rest_ref, late, width - cut)

    def rest_soon(c):
        arrived(rest_out, c, rest_out.wait_remote)
        turn_back(c, rest_rows, rest_ref, soon, cut)

    def mix(matrix_ref, held, i):
        total = jnp.dot(matrix_ref[0], held[i, 0], preferred_element_type=jnp.float32)
        for q in range(1, groups):
            total += jnp.dot(matrix_ref[q], held[i, q], preferred_element_type=jnp.float32)
        return total.reshape(groups, -1, total.shape[1])[:, :pairs]

    def weigh(i, taken, given, held, image, kept):
        taken.wait(i)

        @pl.when(i >= SLOTS)
        def _():
            given.sent(i - SLOTS)

        weighted = mix(metric_ref, held, i)
        half = weighted.astype(jnp.bfloat16)
        image[slot(i)] = half
        given.start(i)
        active = mix(active_ref, held, i) - shift_ref[0] * (weighted - half.astype(jnp.float32))
        kept[i] = active.astype(kept.dtype)
        given.own(i).wait()

    def feed(j):
        @pl.when(j < items)
        def _():
            late_in.start(j)

        @pl.when((j >= items) & (j < 2 * items))
        def _():
            soon_in.start(j - items)

    def weigh_late(i):
        feed(i + WINDOW)
        weigh(i, late_in, late_out, late_held, late_image, late_kept)

    def weigh_soon(i):
        feed(items + i + WINDOW)
        weigh(i, soon_in, soon_out, soon_held, soon_image, soon_kept)

    def combine(i):
        @pl.when(i + WINDOW < items)
        def _():
            front_in.start(i + WINDOW)

        front_in.wait(i)

        @pl.when(i >= SLOTS)
        def _():
            rest_out.sent(i - SLOTS)

        total = soon_kept[i].astype(jnp.float32) + mix(metric_ref, front_held, i)
        rest_made[slot(i)] = total.astype(jnp.bfloat16)
        rest_out.start(i)
        kept_out.start(i)
        rest_out.own(i).wait()

    def load_trial(c):
        return pltpu.make_async_copy(trial_ref.at[:, strip(c), :], flat.at[lax.rem(c, 2)], loaded.at[lax.rem(c, 2)])

    def store_rows(c):
        return pltpu.make_async_copy(turned.at[lax.rem(c, 2)], trial_rows.at[strip(c)], stored.at[lax.rem(c, 2)])

    def turn_trial(c):
        @pl.when(c < chunks)
        def _():
            load_trial(c).wait()
            to_rows(lax.rem(c, 2), width)
            store_rows(c).start()

        @pl.when(c + 2 < chunks)
        def _():
            load_trial(c + 2).start()

        @pl.when(c >= 1)
        def _():
            store_rows(c - 1).wait()
            run((c - 1) * per_chunk, jnp.minimum(c * per_chunk, min(WINDOW, items)), late_in.start)

    def turn_front(c):
        load = pltpu.make_async_copy(
            front_ref.at[:, strip(c), :], flat.at[0, :, :, soon], loaded.at[0])
        load.start()
        load.wait()
        to_rows(0, cut)
        store = pltpu.make_async_copy(turned.at[0, :, :, soon], front_rows.at[strip(c)], stored.at[0])
        store.start()
        store.wait()

    def count(value, most):
        return jnp.clip(value, 0, most)

    for c in range(min(2, chunks)):
        load_trial(c).start()
    pl.semaphore_wait(barrier, peers + groups - 2)
    front.launch_first()
    run(0, chunks + 1, turn_trial)
    run(items, WINDOW, feed)

    late_step = -(-items // max(1, rounds - 3))
    late_ticks = -(-items // late_step)

    def weighed_late(r):
        return count((r + 1) * late_step, items)

    def image_done(r):
        ready = count((r - 1) * late_step, items)
        return jnp.where(ready == items, chunks, ready // per_chunk)

    def weighed_early(r):
        return count((r + 1 - late_ticks) * late_step, items)

    def first_tick(r):
        front.launch_next(r)
        run(weighed_late(r - 1), weighed_late(r), weigh_late)
        run(weighed_early(r - 1), weighed_early(r), weigh_soon)
        run(image_done(r - 1), image_done(r), image_late)
        front.apply(r)

    run(0, rounds, first_tick)
    run(weighed_late(rounds - 1), items, weigh_late)
    run(image_done(rounds - 1), chunks, image_late)
    back.launch_first()

    soon_step = 2 * late_step
    begun = weighed_early(rounds - 1)

    def weighed_soon(r):
        return count(begun + (r + 1) * soon_step, items)

    def combined(r):
        return count((r - 3) * 5 // 2, items)

    def soon_done(r):
        return count(r - 3, chunks)

    def late_done(r):
        return count((r - 8) * 2, chunks)

    def second_tick(r):
        back.launch_next(r)
        run(weighed_soon(r - 1), weighed_soon(r), weigh_soon)

        @pl.when(r == 1)
        def _():
            front.settle()
            run(0, chunks, turn_front)
            run(0, min(WINDOW, items), front_in.start)

        run(combined(r - 1), combined(r), combine)
        run(soon_done(r - 1), soon_done(r), image_soon)
        run(late_done(r - 1), late_done(r), rest_late)
        back.apply(r)

    run(0, rounds, second_tick)
    last = rounds - 1
    run(weighed_soon(last), items, weigh_soon)
    run(combined(last), items, combine)
    run(soon_done(last), chunks, image_soon)
    run(late_done(last), chunks, rest_late)
    run(0, chunks, rest_soon)
    back.settle()
    front.drain()
    back.drain()
    late_in.drain(0)
    soon_in.drain(0)
    kept_out.drain(0)
    front_in.drain(0)
    for swap in (late_out, soon_out, rest_out):
        swap.drain(max(items - SLOTS, 0))


def sweep(groups, peers, rows, cut, shift, fock, metric, active, trial):
    pairs, padded, width = trial.shape
    items = rows // groups
    rounds = -(-pairs // peers)
    rest = width - cut
    ring = min(rounds, 6)
    tall = groups * items
    whole = pl.BlockSpec(memory_space=pltpu.VMEM)
    anywhere = pl.BlockSpec(memory_space=pl.ANY)
    half, dma = jnp.bfloat16, pltpu.SemaphoreType.DMA

    def made(*shape):
        return jax.ShapeDtypeStruct(shape, half)

    outs = pl.pallas_call(
        functools.partial(main_kernel, groups, peers, rows, cut),
        out_shape=[
            made(padded, pairs, width), made(padded, pairs, width), made(pairs, padded, width),
            made(pairs, padded, cut), made(padded, pairs, cut), made(pairs, padded, rest),
            made(padded, pairs, width), made(pairs, padded, width),
        ],
        in_specs=[pl.BlockSpec(memory_space=pltpu.SMEM)] + [whole] * 3 + [anywhere],
        out_specs=[anywhere] * 8,
        scratch_shapes=[
            pltpu.VMEM((rounds, peers, padded, cut), half),
            pltpu.VMEM((rounds, peers, padded, rest), half),
            pltpu.VMEM((ring, peers, padded, cut), half),
            pltpu.VMEM((ring, peers, padded, rest), half),
            pltpu.VMEM((items, groups, pairs, rest), half),
            pltpu.VMEM((items, groups, pairs, cut), half),
            pltpu.VMEM((items, groups, pairs, cut), half),
            pltpu.VMEM((SLOTS, groups, pairs, rest), half),
            pltpu.VMEM((SLOTS, groups, pairs, cut), half),
            pltpu.VMEM((items, groups, pairs, rest), half),
            pltpu.VMEM((items, groups, pairs, cut), half),
            pltpu.VMEM((SLOTS, groups, pairs, cut), half),
            pltpu.VMEM((2, pairs, HIGH, width), half),
            pltpu.VMEM((2, HIGH, pairs, width), half),
            dma((4, rounds, peers)), dma((4, rounds, peers)), dma((7, 2, items, groups)), dma((2,)), dma((2,)),
        ],
        compiler_params=pltpu.CompilerParams(
            collective_id=1, has_side_effects=True, vmem_limit_bytes=63 * 2**20),
    )(shift, fock, metric, active, trial)
    return outs[2], outs[5], outs[7]


def finish_kernel(groups, peers, fock_ref, trial_ref, image_ref, left_ref, rest_ref, out_ref, stats_ref,
                  trial, image, left, rest, sigma, part, slots, loaded, stored, sent, landed):
    group, me = lax.axis_index("act"), lax.axis_index("virt")
    count = groups * peers
    mine = group * peers + me
    barrier = pltpu.get_barrier_semaphore()
    chunks = loaded.shape[1]
    depth = trial.shape[0] // chunks
    rows, width = trial.shape[1], trial.shape[2]
    tail = left.shape[2]
    cut = width - tail

    def span(c):
        return pl.ds(c * depth, depth)

    def load(c, which):
        source, target = ((trial_ref, trial), (image_ref, image), (left_ref, left), (rest_ref, rest))[which]
        return pltpu.make_async_copy(source.at[span(c)], target.at[span(c)], loaded.at[which, c])

    def load_all(c, carry):
        for which in range(4):
            load(c, which).start()
        return carry

    lax.fori_loop(0, chunks, load_all, 0)

    def target(step):
        other = lax.rem(mine + step, count)
        return other, (other // peers, lax.rem(other, peers))

    def greet(step, carry):
        pl.semaphore_signal(barrier, inc=1, device_id=target(step)[1], device_id_type=MESH)
        return carry

    lax.fori_loop(1, count, greet, 0)

    def product(c, carry):
        numer, denom = carry
        for which in range(4):
            load(c, which).wait()
        own = image[span(c)].reshape(depth * rows, width)
        total = jnp.dot(own, fock_ref[...], preferred_element_type=jnp.float32)
        total += rest[span(c)].reshape(depth * rows, width).astype(jnp.float32)
        last = total[:, cut:] + left[span(c)].reshape(depth * rows, tail).astype(jnp.float32)
        total = jnp.concatenate([total[:, :cut], last], axis=1)
        sigma[span(c)] = total.reshape(depth, rows, width)
        wide = trial[span(c)].reshape(depth * rows, width).astype(jnp.float32)
        numer += jnp.sum(wide * total, axis=0, keepdims=True)
        denom += jnp.sum(wide * own.astype(jnp.float32), axis=0, keepdims=True)
        return numer, denom

    zero = jnp.zeros((1, width), jnp.float32)
    numer, denom = lax.fori_loop(0, chunks, product, (zero, zero))
    pl.semaphore_wait(barrier, count - 1)

    def sum_all(phase, value):
        part[phase] = value

        def copy(step, slot):
            other, place = target(step)
            return pltpu.make_async_remote_copy(
                src_ref=part.at[phase], dst_ref=slots.at[phase, slot],
                send_sem=sent.at[phase, other], recv_sem=landed.at[phase, slot],
                device_id=place, device_id_type=MESH)

        def send(step, carry):
            copy(step, mine).start()
            return carry

        lax.fori_loop(1, count, send, 0)
        slots[phase, mine] = value

        def receive(step, carry):
            copy(step, target(step)[0]).wait_recv()
            return carry

        lax.fori_loop(1, count, receive, 0)

        def finish(step, carry):
            copy(step, mine).wait_send()
            return carry

        lax.fori_loop(1, count, finish, 0)
        return jnp.sum(slots[phase], axis=0)

    row = lax.broadcasted_iota(jnp.int32, (8, 128), 0)
    numer_one = jnp.sum(numer, axis=1, keepdims=True)
    denom_one = jnp.sum(denom, axis=1, keepdims=True)
    sums = sum_all(0, jnp.where(row == 0, numer_one, denom_one))
    denominator = sums[1:2, 0:1]
    rayleigh = sums[0:1, 0:1] / denominator

    def store(c):
        return pltpu.make_async_copy(rest.at[span(c)], out_ref.at[span(c)], stored.at[c])

    def residual(c, squares):
        own = image[span(c)].reshape(depth * rows, width).astype(jnp.float32)
        resid = sigma[span(c)].reshape(depth * rows, width) - rayleigh * own
        rest[span(c)] = resid.astype(jnp.bfloat16).reshape(depth, rows, width)
        store(c).start()
        return squares + jnp.sum(resid * resid, axis=0, keepdims=True)

    squares = lax.fori_loop(0, chunks, residual, zero)
    square_one = jnp.sum(squares, axis=1, keepdims=True)
    norms = sum_all(1, jnp.broadcast_to(square_one, (8, 128)))
    stats_ref[...] = jnp.where(row == 0, rayleigh, norms / denominator)

    def drain(c, carry):
        store(c).wait()
        return carry

    lax.fori_loop(0, chunks, drain, 0)


def finish(groups, peers, fock, trial, image, left, rest):
    pairs, rows, width = trial.shape
    depth = next(d for d in (5, 4, 2, 1) if pairs % d == 0)
    chunks = pairs // depth
    whole = pl.BlockSpec(memory_space=pltpu.VMEM)
    anywhere = pl.BlockSpec(memory_space=pl.ANY)
    dma = pltpu.SemaphoreType.DMA
    count = groups * peers
    return pl.pallas_call(
        functools.partial(finish_kernel, groups, peers),
        out_shape=[
            jax.ShapeDtypeStruct((pairs, rows, width), jnp.bfloat16),
            jax.ShapeDtypeStruct((8, 128), jnp.float32),
        ],
        in_specs=[whole] + [anywhere] * 4,
        out_specs=[anywhere, whole],
        scratch_shapes=[
            pltpu.VMEM((pairs, rows, width), jnp.bfloat16),
            pltpu.VMEM((pairs, rows, width), jnp.bfloat16),
            pltpu.VMEM((pairs, rows, left.shape[2]), jnp.bfloat16),
            pltpu.VMEM((pairs, rows, width), jnp.bfloat16),
            pltpu.VMEM((pairs, rows, width), jnp.float32),
            pltpu.VMEM((2, 8, 128), jnp.float32),
            pltpu.VMEM((2, count, 8, 128), jnp.float32),
            dma((4, chunks)), dma((chunks,)), dma((2, count)), dma((2, count)),
        ],
        compiler_params=pltpu.CompilerParams(
            collective_id=2, has_side_effects=True, vmem_limit_bytes=63 * 2**20),
    )(fock, trial, image, left, rest)


def local(amplitudes, virtual_fock_block, metric, active_block):
    pairs, rows, width = amplitudes.shape
    peers, groups = lax.axis_size("virt"), lax.axis_size("act")
    fock = virtual_fock_block
    padded = -(-rows // 16) * 16
    room = -pairs % 8
    cut = (2 * width // 5) // 128 * 128

    def widen(array):
        if padded == rows:
            return array
        return jnp.pad(array, ((0, 0), (0, padded - rows), (0, 0)))

    def pair_matrix(array):
        spread = jnp.pad(array.reshape(groups, pairs, groups, pairs), ((0, 0), (0, room), (0, 0), (0, 0)))
        return jnp.transpose(spread, (2, 0, 1, 3)).reshape(groups, groups * (pairs + room), pairs)

    spread = fock
    if padded != rows:
        gap = padded - rows
        spread = jnp.pad(
            fock.reshape(peers, rows, peers, rows), ((0, 0), (0, gap), (0, 0), (0, gap))
        ).reshape(peers * padded, peers * padded)
    metric_parts, active_parts = pair_matrix(metric), pair_matrix(active_block)
    at = lax.broadcasted_iota(jnp.int32, fock.shape, 0)
    across = lax.broadcasted_iota(jnp.int32, fock.shape, 1)
    shift = (2.0 / width) * jnp.sum(jnp.where(at == across, fock.astype(jnp.float32), 0.0))
    trial = widen(amplitudes)
    image, left, rest = sweep(
        groups, peers, rows, cut, shift.reshape(1), spread, metric_parts, active_parts, trial)
    resid, stats = finish(groups, peers, fock, trial, image, left, rest)
    return resid[:, :rows], stats[0, 0], stats[1, 0]


def solution(mesh):
    placed = (P("act", "virt", None), P(), P(), P())
    return jax.shard_map(
        local,
        mesh=mesh,
        in_specs=placed,
        out_specs=(P("act", "virt", None), P(), P()),
        check_vma=False,
    )
```

time: 572 us -> 528 us (0.923)
  local copies, waits for them, and re-layouts: 53.4 us -> 14.4 us
  Pallas kernels: 515 us -> 509 us
    pallas_call x4 -> x0, local copies, waits for them, and re-layouts: 27.4 us -> none  [stage(): pl.pallas_call(functools.partial(stage_kernel, first, peers, groups, pair...]
    unnamed x4 -> x1, local copies, waits for them, and re-layouts: 20.3 us -> 8.79 us
    pallas_call x2 -> x1, Pallas kernels: 475 us -> 468 us  [sweep(): pl.pallas_call(functools.partial(main_kernel, groups, peers, rows, cut),...]
where the time goes in v1:
time: 528 us; the launch traced here: 527 us
  Pallas kernels  509 us (96%)
  local copies, waits for them, and re-layouts  14.4 us (3%)
    pallas_call x1, Pallas kernels, sweep(): pl.pallas_call(functools.partial(main_kernel, groups, peers, rows, cut),...  468 us
    pallas_call x1, Pallas kernels, finish(): pl.pallas_call(functools.partial(finish_kernel, groups, peers), out_shape...  40.8 us

profile of v1, /device:TPU:0, one launch (start us, length us, event | category | flops | bytes accessed | tf_op | source)
XLA Modules:
  0.0 526.8 jit_solution(12443914785850022538)
XLA Ops:
  0.6 1.8 select_reduce_fusion
  3.1 1.3 reshape.22
  4.4 0.1 copy.7
  4.5 0.8 pad.7
  5.3 1.3 reshape.24
  6.6 0.1 copy.8
  6.7 0.8 pad.8
  7.5 468.4 %shard_map.67 = (bf16[80,100,640]{2,1,0:T(8,128)(2,1)}, bf16[80,100,640]{2,1,0:T(8,128)(2,1)}, bf16[100,80,640]{2,1,0:T(8,128)(2,1)}, bf16[100,80,256]{2,1,0:T(8...) custom-call(f32[1]{0:T(128)} %bitcast.shift_ref, ...), custom_call_target="tpu_custom_call" | custom-call | tf_op jit(solution)/shard_map/pallas_call | solution.py:487
  475.9 40.8 %shard_map.68 = (bf16[100,80,640]{2,1,0:T(8,128)(2,1)}, f32[8,128]{1,0:T(8,128)}) custom-call(bf16[640,640]{1,0:T(8,128)(2,1)} %fock_ref.3, bf16[100,80,640]{2,1,0:T(8,128)(2,1)} %trial_ref.3, bf16[100,80,640]{2,1,0:T(8,128)(2,1)} %get-tuple-element.8.image_ref, bf16[100,80,384]{2,1,0:T(8,128)(2,1)} %get-tuple-element.9.left_ref, ...), custom_call_target="tpu_custom_call" | custom-call | tf_op jit(solution)/shard_map/pallas_call | solution.py:641
  516.7 1.3 fusion
  518.0 8.8 %copy.10 = bf16[100,80,640]{2,1,0:T(8,128)(2,1)} copy(bf16[100,80,640]{2,1,0:T(8,128)(2,1)} %get-tuple-element.18) | data formatting | bytes 20480000

commit v2 on v1

--- a/solution.py
+++ b/solution.py
@@ -14,12 +14,19 @@
 HIGH = 16
 SLOTS = 8
 WINDOW = 8
-
-
-def main_kernel(groups, peers, rows, cut, shift_ref, fock_ref, metric_ref, active_ref, trial_ref,
+EARLY = 3
+JOIN = 5
+MERGE = 4
+TALL = 8
+
+
+def main_kernel(groups, peers, rows, cut, spread_ref, metric_in, active_in, fock_ref, trial_ref,
                 trial_rows, image_rows, image_ref, front_ref, front_rows, left_ref, rest_rows, rest_ref,
+                sigma_ref, stats_ref,
                 held_a, held_b, made_a, made_b, late_held, soon_held, front_held, late_image, soon_image,
-                late_kept, soon_kept, rest_made, flat, turned, sems_a, sems_b, act_sems, loaded, stored):
+                late_kept, soon_kept, rest_made, flat, turned, trial, image, rest, left, sigma, sums, part, slots,
+                metric_ref, active_ref, shift_ref,
+                sems_a, sems_b, act_sems, loaded, stored, fetched, written, sent, landed):
     group, me = lax.axis_index("act"), lax.axis_index("virt")
     pairs, padded, width = trial_ref.shape
     rounds = held_a.shape[0]
@@ -28,13 +35,19 @@
     per_chunk = HIGH // groups
     soon, late = pl.ds(0, cut), pl.ds(cut, width - cut)
 
+    mine, devices = group * peers + me, groups * peers
+
+    def target(step):
+        other = lax.rem(mine + step, devices)
+        return other, (other // peers, lax.rem(other, peers))
+
     barrier = pltpu.get_barrier_semaphore()
-    for step in range(1, peers):
-        pl.semaphore_signal(
-            barrier, inc=1, device_id=(group, lax.rem(me + step, peers)), device_id_type=MESH)
-    for step in range(1, groups):
-        pl.semaphore_signal(
-            barrier, inc=1, device_id=(lax.rem(group + step, groups), me), device_id_type=MESH)
+
+    def greet(step, carry):
+        pl.semaphore_signal(barrier, inc=1, device_id=target(step)[1], device_id_type=MESH)
+        return carry
+
+    lax.fori_loop(1, devices, greet, 0)
 
     whole_rounds = pairs // peers
     spare = pairs % peers
@@ -129,29 +142,25 @@
                     self.sent_back(r - self.ring)
 
                 block = self.held[r].reshape(peers * padded, self.held.shape[3])
-                product = jnp.dot(fock_ref[...], block, preferred_element_type=jnp.float32)
+                product = jnp.dot(spread_ref[...], block, preferred_element_type=jnp.float32)
                 self.made[lax.rem(r, self.ring)] = product.astype(jnp.bfloat16).reshape(
                     peers, padded, self.held.shape[3])
                 self.backward_own(r).start()
                 for step in range(1, peers):
                     self.backward(r, lax.rem(me + step, peers)).start()
 
-        def settle(self):
+        def settle_own(self):
             @pl.when(owns(rounds - 1, me))
             def _():
                 self.backward_own(rounds - 1).wait()
 
-            def landed(r, carry):
-                for step in range(1, peers):
-                    peer = lax.rem(me + step, peers)
-
-                    @pl.when(owns(r, peer))
-                    def _(peer=peer):
-                        self.back_arrival(r, peer).wait_recv()
-
-                return carry
-
-            lax.fori_loop(0, rounds, landed, 0)
+        def settle(self, r):
+            for step in range(1, peers):
+                peer = lax.rem(me + step, peers)
+
+                @pl.when(owns(r, peer))
+                def _(peer=peer):
+                    self.back_arrival(r, peer).wait_recv()
 
         def drain(self):
             def done(r, carry):
@@ -306,20 +315,31 @@
             total += jnp.dot(matrix_ref[q], held[i, q], preferred_element_type=jnp.float32)
         return total.reshape(groups, -1, total.shape[1])[:, :pairs]
 
+    def settled(swap, i):
+        @pl.when(i >= 1)
+        def _():
+            swap.own(i - 1).wait()
+
+        @pl.when(i >= SLOTS)
+        def _():
+            swap.sent(i - SLOTS)
+
+    def closed(swap, i):
+        @pl.when(i == items - 1)
+        def _():
+            swap.own(i).wait()
+
     def weigh(i, taken, given, held, image, kept):
         taken.wait(i)
-
-        @pl.when(i >= SLOTS)
-        def _():
-            given.sent(i - SLOTS)
+        settled(given, i)
 
         weighted = mix(metric_ref, held, i)
         half = weighted.astype(jnp.bfloat16)
         image[slot(i)] = half
         given.start(i)
-        active = mix(active_ref, held, i) - shift_ref[0] * (weighted - half.astype(jnp.float32))
+        active = mix(active_ref, held, i) - shift_ref[...] * (weighted - half.astype(jnp.float32))
         kept[i] = active.astype(kept.dtype)
-        given.own(i).wait()
+        closed(given, i)
 
     def feed(j):
         @pl.when(j < items)
@@ -337,6 +357,7 @@
     def weigh_soon(i):
         feed(items + i + WINDOW)
         weigh(i, soon_in, soon_out, soon_held, soon_image, soon_kept)
+        kept_out.start(i)
 
     def combine(i):
         @pl.when(i + WINDOW < items)
@@ -344,16 +365,12 @@
             front_in.start(i + WINDOW)
 
         front_in.wait(i)
-
-        @pl.when(i >= SLOTS)
-        def _():
-            rest_out.sent(i - SLOTS)
+        settled(rest_out, i)
 
         total = soon_kept[i].astype(jnp.float32) + mix(metric_ref, front_held, i)
         rest_made[slot(i)] = total.astype(jnp.bfloat16)
         rest_out.start(i)
-        kept_out.start(i)
-        rest_out.own(i).wait()
+        closed(rest_out, i)
 
     def load_trial(c):
         return pltpu.make_async_copy(trial_ref.at[:, strip(c), :], flat.at[lax.rem(c, 2)], loaded.at[lax.rem(c, 2)])
@@ -387,55 +404,178 @@
         store.start()
         store.wait()
 
+    depth = trial.shape[1]
+    spans = pairs // depth
+
+    def span(c):
+        return pl.ds(c * depth, depth)
+
+    def fetches(c):
+        at = lax.rem(c, 2)
+        return [
+            pltpu.make_async_copy(source.at[span(c)], place.at[at], fetched.at[which, at])
+            for which, (source, place) in enumerate(
+                ((trial_ref, trial), (image_ref, image), (rest_ref, rest)))]
+
+    def fetch_left(c):
+        at = lax.rem(c, 2)
+        return pltpu.make_async_copy(left_ref.at[span(c)], left.at[at], fetched.at[3, at])
+
+    def write(c):
+        at = lax.rem(c, 2)
+        return pltpu.make_async_copy(sigma.at[at], sigma_ref.at[span(c)], written.at[at])
+
+    def total(value):
+        return jnp.sum(value, axis=0, keepdims=True)
+
+    def join(c):
+        at = lax.rem(c, 2)
+
+        @pl.when(lax.rem(c * depth, peers) == 0)
+        def _():
+            back.settle(c * depth // peers)
+
+        fetch_left(c).start()
+
+        @pl.when(c + 1 < spans)
+        def _():
+            for copy in fetches(c + 1):
+                copy.start()
+
+        for copy in fetches(c):
+            copy.wait()
+
+        @pl.when(c >= 2)
+        def _():
+            write(c - 2).wait()
+
+        own = image[at].reshape(depth * padded, width)
+        sums_of = jnp.dot(own, fock_ref[...], preferred_element_type=jnp.float32)
+        sums_of += rest[at].reshape(depth * padded, width).astype(jnp.float32)
+        fetch_left(c).wait()
+        tail = sums_of[:, cut:] + left[at].reshape(depth * padded, width - cut).astype(jnp.float32)
+        sums_of = jnp.concatenate([sums_of[:, :cut], tail], axis=1)
+        own = own.astype(jnp.float32)
+        wide = trial[at].reshape(depth * padded, width).astype(jnp.float32)
+        apart = sums_of - shift_ref[...] * own
+        sigma[at] = apart.astype(jnp.bfloat16).reshape(depth, padded, width)
+        write(c).start()
+        sums[0:1] += total(wide * apart)
+        sums[1:2] += total(wide * own)
+        sums[2:3] += total(apart * apart)
+        sums[3:4] += total(apart * own)
+        sums[4:5] += total(own * own)
+
+    def gather(value):
+        part[...] = value
+
+        def copy(step, at):
+            other, place = target(step)
+            return pltpu.make_async_remote_copy(
+                src_ref=part, dst_ref=slots.at[at], send_sem=sent.at[other], recv_sem=landed.at[at],
+                device_id=place, device_id_type=MESH)
+
+        def send(step, carry):
+            copy(step, mine).start()
+            return carry
+
+        lax.fori_loop(1, devices, send, 0)
+        slots[mine] = value
+
+        def receive(step, carry):
+            copy(step, target(step)[0]).wait_recv()
+            return carry
+
+        lax.fori_loop(1, devices, receive, 0)
+
+        def done(step, carry):
+            copy(step, mine).wait_send()
+            return carry
+
+        lax.fori_loop(1, devices, done, 0)
+        return jnp.sum(slots[...], axis=0)
+
+    def finish():
+        sums[...] = jnp.zeros_like(sums)
+        for copy in fetches(0):
+            copy.start()
+        run(0, spans, join)
+        found = jnp.sum(sums[...], axis=1, keepdims=True)
+        found = gather(jnp.broadcast_to(found, (8, 128)))
+        denominator = found[1:2]
+        over = found[0:1] / denominator
+        squares = found[2:3] - 2.0 * over * found[3:4] + over * over * found[4:5]
+        at = lax.broadcasted_iota(jnp.int32, (8, 128), 0)
+        stats_ref[...] = jnp.where(
+            at == 0, shift_ref[...] + over, jnp.where(at == 1, squares / denominator, over))
+        for c in range(max(spans - 2, 0), spans):
+            write(c).wait()
+
+    def prepare():
+        tall = metric_ref.shape[1] // groups
+        for source, place in ((metric_in, metric_ref), (active_in, active_ref)):
+            place[...] = jnp.zeros_like(place)
+            for q in range(groups):
+                for p in range(groups):
+                    place[q, pl.ds(p * tall, pairs), :] = source[pl.ds(p * pairs, pairs), pl.ds(q * pairs, pairs)]
+        at = lax.broadcasted_iota(jnp.int32, fock_ref.shape, 0)
+        across = lax.broadcasted_iota(jnp.int32, fock_ref.shape, 1)
+        diagonal = jnp.where(at == across, fock_ref[...].astype(jnp.float32), 0.0)
+        shift_ref[...] = (2.0 / width) * jnp.sum(jnp.sum(diagonal, axis=0, keepdims=True), axis=1, keepdims=True)
+
     def count(value, most):
         return jnp.clip(value, 0, most)
 
     for c in range(min(2, chunks)):
         load_trial(c).start()
-    pl.semaphore_wait(barrier, peers + groups - 2)
+    pl.semaphore_wait(barrier, devices - 1)
     front.launch_first()
     run(0, chunks + 1, turn_trial)
+    prepare()
     run(items, WINDOW, feed)
 
-    late_step = -(-items // max(1, rounds - 3))
-    late_ticks = -(-items // late_step)
+    late_ticks = max(1, rounds - 2)
 
     def weighed_late(r):
-        return count((r + 1) * late_step, items)
+        return count(((r + 1) * items + late_ticks // 2) // late_ticks, items)
 
     def image_done(r):
-        ready = count((r - 1) * late_step, items)
+        ready = jnp.where(r >= 1, weighed_late(r - 1), 0)
         return jnp.where(ready == items, chunks, ready // per_chunk)
 
     def weighed_early(r):
-        return count((r + 1 - late_ticks) * late_step, items)
+        return count((r + 2 - rounds) * EARLY, items)
 
     def first_tick(r):
         front.launch_next(r)
         run(weighed_late(r - 1), weighed_late(r), weigh_late)
         run(weighed_early(r - 1), weighed_early(r), weigh_soon)
         run(image_done(r - 1), image_done(r), image_late)
+
+        @pl.when(r == rounds - 1)
+        def _():
+            run(image_done(r), chunks, image_late)
+            back.launch_first()
+
         front.apply(r)
 
     run(0, rounds, first_tick)
-    run(weighed_late(rounds - 1), items, weigh_late)
-    run(image_done(rounds - 1), chunks, image_late)
-    back.launch_first()
-
-    soon_step = 2 * late_step
     begun = weighed_early(rounds - 1)
 
     def weighed_soon(r):
-        return count(begun + (r + 1) * soon_step, items)
+        return count(begun + (r + 1) * EARLY, items)
 
     def combined(r):
-        return count((r - 3) * 5 // 2, items)
+        return count((r + 1 - JOIN) * MERGE, items)
 
     def soon_done(r):
-        return count(r - 3, chunks)
+        return count(jnp.where(weighed_soon(r - 1) == items, chunks, weighed_soon(r - 1) // per_chunk), chunks)
 
     def late_done(r):
-        return count((r - 8) * 2, chunks)
+        return jnp.where(r >= 1, soon_done(r - 1), 0)
+
+    def rest_done(r):
+        return combined(r - 1) // per_chunk
 
     def second_tick(r):
         back.launch_next(r)
@@ -443,23 +583,29 @@
 
         @pl.when(r == 1)
         def _():
-            front.settle()
+            front.settle_own()
+            run(0, rounds, front.settle)
             run(0, chunks, turn_front)
             run(0, min(WINDOW, items), front_in.start)
 
         run(combined(r - 1), combined(r), combine)
         run(soon_done(r - 1), soon_done(r), image_soon)
         run(late_done(r - 1), late_done(r), rest_late)
+        run(rest_done(r - 1), rest_done(r), rest_soon)
         back.apply(r)
 
     run(0, rounds, second_tick)
     last = rounds - 1
     run(weighed_soon(last), items, weigh_soon)
-    run(combined(last), items, combine)
     run(soon_done(last), chunks, image_soon)
     run(late_done(last), chunks, rest_late)
-    run(0, chunks, rest_soon)
-    back.settle()
+    most = min(items, (chunks - 1) * per_chunk + 1)
+    run(combined(last), most, combine)
+    run(rest_done(last), chunks - 1, rest_soon)
+    run(jnp.maximum(combined(last), most), items, combine)
+    run(jnp.maximum(rest_done(last), chunks - 1), chunks, rest_soon)
+    back.settle_own()
+    finish()
     front.drain()
     back.drain()
     late_in.drain(0)
@@ -470,13 +616,14 @@
         swap.drain(max(items - SLOTS, 0))
 
 
-def sweep(groups, peers, rows, cut, shift, fock, metric, active, trial):
+def sweep(groups, peers, rows, cut, spread, metric, active, fock, trial):
     pairs, padded, width = trial.shape
     items = rows // groups
     rounds = -(-pairs // peers)
     rest = width - cut
     ring = min(rounds, 6)
-    tall = groups * items
+    devices, tall = groups * peers, -(-pairs // TALL) * TALL
+    depth = next(d for d in (4, 2, 1) if pairs % d == 0 and peers % d == 0)
     whole = pl.BlockSpec(memory_space=pltpu.VMEM)
     anywhere = pl.BlockSpec(memory_space=pl.ANY)
     half, dma = jnp.bfloat16, pltpu.SemaphoreType.DMA
@@ -490,9 +637,11 @@
             made(padded, pairs, width), made(padded, pairs, width), made(pairs, padded, width),
             made(pairs, padded, cut), made(padded, pairs, cut), made(pairs, padded, rest),
             made(padded, pairs, width), made(pairs, padded, width),
+            made(pairs, padded, width),
+            jax.ShapeDtypeStruct((8, 128), jnp.float32),
         ],
-        in_specs=[pl.BlockSpec(memory_space=pltpu.SMEM)] + [whole] * 3 + [anywhere],
-        out_specs=[anywhere] * 8,
+        in_specs=[whole] * 4 + [anywhere],
+        out_specs=[anywhere] * 9 + [whole],
         scratch_shapes=[
             pltpu.VMEM((rounds, peers, padded, cut), half),
             pltpu.VMEM((rounds, peers, padded, rest), half),
@@ -508,157 +657,78 @@
             pltpu.VMEM((SLOTS, groups, pairs, cut), half),
             pltpu.VMEM((2, pairs, HIGH, width), half),
             pltpu.VMEM((2, HIGH, pairs, width), half),
+            pltpu.VMEM((2, depth, padded, width), half),
+            pltpu.VMEM((2, depth, padded, width), half),
+            pltpu.VMEM((2, depth, padded, width), half),
+            pltpu.VMEM((2, depth, padded, rest), half),
+            pltpu.VMEM((2, depth, padded, width), half),
+            pltpu.VMEM((8, width), jnp.float32),
+            pltpu.VMEM((8, 128), jnp.float32),
+            pltpu.VMEM((devices, 8, 128), jnp.float32),
+            pltpu.VMEM((groups, groups * tall, pairs), half),
+            pltpu.VMEM((groups, groups * tall, pairs), half),
+            pltpu.VMEM((1, 1), jnp.float32),
             dma((4, rounds, peers)), dma((4, rounds, peers)), dma((7, 2, items, groups)), dma((2,)), dma((2,)),
+            dma((4, 2)), dma((2,)), dma((devices,)), dma((devices,)),
         ],
         compiler_params=pltpu.CompilerParams(
             collective_id=1, has_side_effects=True, vmem_limit_bytes=63 * 2**20),
-    )(shift, fock, metric, active, trial)
-    return outs[2], outs[5], outs[7]
-
-
-def finish_kernel(groups, peers, fock_ref, trial_ref, image_ref, left_ref, rest_ref, out_ref, stats_ref,
-                  trial, image, left, rest, sigma, part, slots, loaded, stored, sent, landed):
-    group, me = lax.axis_index("act"), lax.axis_index("virt")
-    count = groups * peers
-    mine = group * peers + me
-    barrier = pltpu.get_barrier_semaphore()
+    )(spread, metric, active, fock, trial)
+    return outs[2], outs[8], outs[9]
+
+
+def close_kernel(stats_ref, apart_ref, image_ref, out_ref, apart, image, loaded, stored):
     chunks = loaded.shape[1]
-    depth = trial.shape[0] // chunks
-    rows, width = trial.shape[1], trial.shape[2]
-    tail = left.shape[2]
-    cut = width - tail
+    depth = apart.shape[0] // chunks
+    over = stats_ref[2:3, 0:1].reshape(1, 1, 1)
 
     def span(c):
         return pl.ds(c * depth, depth)
 
-    def load(c, which):
-        source, target = ((trial_ref, trial), (image_ref, image), (left_ref, left), (rest_ref, rest))[which]
-        return pltpu.make_async_copy(source.at[span(c)], target.at[span(c)], loaded.at[which, c])
-
-    def load_all(c, carry):
-        for which in range(4):
-            load(c, which).start()
+    def loads(c):
+        return (pltpu.make_async_copy(apart_ref.at[span(c)], apart.at[span(c)], loaded.at[0, c]),
+                pltpu.make_async_copy(image_ref.at[span(c)], image.at[span(c)], loaded.at[1, c]))
+
+    def store(c):
+        return pltpu.make_async_copy(apart.at[span(c)], out_ref.at[span(c)], stored.at[c])
+
+    def begin(c, carry):
+        for copy in loads(c):
+            copy.start()
         return carry
 
-    lax.fori_loop(0, chunks, load_all, 0)
-
-    def target(step):
-        other = lax.rem(mine + step, count)
-        return other, (other // peers, lax.rem(other, peers))
-
-    def greet(step, carry):
-        pl.semaphore_signal(barrier, inc=1, device_id=target(step)[1], device_id_type=MESH)
+    def close_one(c, carry):
+        for copy in loads(c):
+            copy.wait()
+        resid = apart[span(c)].astype(jnp.float32) - over * image[span(c)].astype(jnp.float32)
+        apart[span(c)] = resid.astype(apart.dtype)
+        store(c).start()
         return carry
 
-    lax.fori_loop(1, count, greet, 0)
-
-    def product(c, carry):
-        numer, denom = carry
-        for which in range(4):
-            load(c, which).wait()
-        own = image[span(c)].reshape(depth * rows, width)
-        total = jnp.dot(own, fock_ref[...], preferred_element_type=jnp.float32)
-        total += rest[span(c)].reshape(depth * rows, width).astype(jnp.float32)
-        last = total[:, cut:] + left[span(c)].reshape(depth * rows, tail).astype(jnp.float32)
-        total = jnp.concatenate([total[:, :cut], last], axis=1)
-        sigma[span(c)] = total.reshape(depth, rows, width)
-        wide = trial[span(c)].reshape(depth * rows, width).astype(jnp.float32)
-        numer += jnp.sum(wide * total, axis=0, keepdims=True)
-        denom += jnp.sum(wide * own.astype(jnp.float32), axis=0, keepdims=True)
-        return numer, denom
-
-    zero = jnp.zeros((1, width), jnp.float32)
-    numer, denom = lax.fori_loop(0, chunks, product, (zero, zero))
-    pl.semaphore_wait(barrier, count - 1)
-
-    def sum_all(phase, value):
-        part[phase] = value
-
-        def copy(step, slot):
-            other, place = target(step)
-            return pltpu.make_async_remote_copy(
-                src_ref=part.at[phase], dst_ref=slots.at[phase, slot],
-                send_sem=sent.at[phase, other], recv_sem=landed.at[phase, slot],
-                device_id=place, device_id_type=MESH)
-
-        def send(step, carry):
-            copy(step, mine).start()
-            return carry
-
-        lax.fori_loop(1, count, send, 0)
-        slots[phase, mine] = value
-
-        def receive(step, carry):
-            copy(step, target(step)[0]).wait_recv()
-            return carry
-
-        lax.fori_loop(1, count, receive, 0)
-
-        def finish(step, carry):
-            copy(step, mine).wait_send()
-            return carry
-
-        lax.fori_loop(1, count, finish, 0)
-        return jnp.sum(slots[phase], axis=0)
-
-    row = lax.broadcasted_iota(jnp.int32, (8, 128), 0)
-    numer_one = jnp.sum(numer, axis=1, keepdims=True)
-    denom_one = jnp.sum(denom, axis=1, keepdims=True)
-    sums = sum_all(0, jnp.where(row == 0, numer_one, denom_one))
-    denominator = sums[1:2, 0:1]
-    rayleigh = sums[0:1, 0:1] / denominator
-
-    def store(c):
-        return pltpu.make_async_copy(rest.at[span(c)], out_ref.at[span(c)], stored.at[c])
-
-    def residual(c, squares):
-        own = image[span(c)].reshape(depth * rows, width).astype(jnp.float32)
-        resid = sigma[span(c)].reshape(depth * rows, width) - rayleigh * own
-        rest[span(c)] = resid.astype(jnp.bfloat16).reshape(depth, rows, width)
-        store(c).start()
-        return squares + jnp.sum(resid * resid, axis=0, keepdims=True)
-
-    squares = lax.fori_loop(0, chunks, residual, zero)
-    square_one = jnp.sum(squares, axis=1, keepdims=True)
-    norms = sum_all(1, jnp.broadcast_to(square_one, (8, 128)))
-    stats_ref[...] = jnp.where(row == 0, rayleigh, norms / denominator)
-
-    def drain(c, carry):
+    def end(c, carry):
         store(c).wait()
         return carry
 
-    lax.fori_loop(0, chunks, drain, 0)
-
-
-def finish(groups, peers, fock, trial, image, left, rest):
-    pairs, rows, width = trial.shape
+    for work in (begin, close_one, end):
+        lax.fori_loop(0, chunks, work, 0)
+
+
+def close(stats, apart, image):
+    pairs, padded, width = apart.shape
     depth = next(d for d in (5, 4, 2, 1) if pairs % d == 0)
-    chunks = pairs // depth
-    whole = pl.BlockSpec(memory_space=pltpu.VMEM)
     anywhere = pl.BlockSpec(memory_space=pl.ANY)
     dma = pltpu.SemaphoreType.DMA
-    count = groups * peers
     return pl.pallas_call(
-        functools.partial(finish_kernel, groups, peers),
-        out_shape=[
-            jax.ShapeDtypeStruct((pairs, rows, width), jnp.bfloat16),
-            jax.ShapeDtypeStruct((8, 128), jnp.float32),
+        close_kernel,
+        out_shape=jax.ShapeDtypeStruct(image.shape, image.dtype),
+        in_specs=[pl.BlockSpec(memory_space=pltpu.VMEM), anywhere, anywhere],
+        out_specs=anywhere,
+        scratch_shapes=[
+            pltpu.VMEM(apart.shape, apart.dtype), pltpu.VMEM(image.shape, image.dtype),
+            dma((2, pairs // depth)), dma((pairs // depth,)),
         ],
-        in_specs=[whole] + [anywhere] * 4,
-        out_specs=[anywhere, whole],
-        scratch_shapes=[
-            pltpu.VMEM((pairs, rows, width), jnp.bfloat16),
-            pltpu.VMEM((pairs, rows, width), jnp.bfloat16),
-            pltpu.VMEM((pairs, rows, left.shape[2]), jnp.bfloat16),
-            pltpu.VMEM((pairs, rows, width), jnp.bfloat16),
-            pltpu.VMEM((pairs, rows, width), jnp.float32),
-            pltpu.VMEM((2, 8, 128), jnp.float32),
-            pltpu.VMEM((2, count, 8, 128), jnp.float32),
-            dma((4, chunks)), dma((chunks,)), dma((2, count)), dma((2, count)),
-        ],
-        compiler_params=pltpu.CompilerParams(
-            collective_id=2, has_side_effects=True, vmem_limit_bytes=63 * 2**20),
-    )(fock, trial, image, left, rest)
+        compiler_params=pltpu.CompilerParams(vmem_limit_bytes=60 * 2**20),
+    )(stats, apart, image)
 
 
 def local(amplitudes, virtual_fock_block, metric, active_block):
@@ -666,17 +736,12 @@
     peers, groups = lax.axis_size("virt"), lax.axis_size("act")
     fock = virtual_fock_block
     padded = -(-rows // 16) * 16
-    room = -pairs % 8
     cut = (2 * width // 5) // 128 * 128
 
     def widen(array):
         if padded == rows:
             return array
         return jnp.pad(array, ((0, 0), (0, padded - rows), (0, 0)))
-
-    def pair_matrix(array):
-        spread = jnp.pad(array.reshape(groups, pairs, groups, pairs), ((0, 0), (0, room), (0, 0), (0, 0)))
-        return jnp.transpose(spread, (2, 0, 1, 3)).reshape(groups, groups * (pairs + room), pairs)
 
     spread = fock
     if padded != rows:
@@ -684,14 +749,10 @@
         spread = jnp.pad(
             fock.reshape(peers, rows, peers, rows), ((0, 0), (0, gap), (0, 0), (0, gap))
         ).reshape(peers * padded, peers * padded)
-    metric_parts, active_parts = pair_matrix(metric), pair_matrix(active_block)
-    at = lax.broadcasted_iota(jnp.int32, fock.shape, 0)
-    across = lax.broadcasted_iota(jnp.int32, fock.shape, 1)
-    shift = (2.0 / width) * jnp.sum(jnp.where(at == across, fock.astype(jnp.float32), 0.0))
     trial = widen(amplitudes)
-    image, left, rest = sweep(
-        groups, peers, rows, cut, shift.reshape(1), spread, metric_parts, active_parts, trial)
-    resid, stats = finish(groups, peers, fock, trial, image, left, rest)
+    image, sigma, stats = sweep(
+        groups, peers, rows, cut, spread, metric, active_block, fock, trial)
+    resid = close(stats, sigma, image)
     return resid[:, :rows], stats[0, 0], stats[1, 0]
 
 

time: 528 us -> 513 us (0.972)
  local copies, waits for them, and re-layouts: 14.4 us -> 1.27 us
    pallas_call x1, Pallas kernels: 468 us -> 497 us  [sweep(): pl.pallas_call(functools.partial(main_kernel, groups, peers, rows, cut),...]
    pallas_call x1, Pallas kernels: 40.8 us -> 12.1 us  [close(): pl.pallas_call(close_kernel, out_shape=jax.ShapeDtypeStruct(image.shape,...]
    unnamed x1 -> x0, local copies, waits for them, and re-layouts: 8.79 us -> none
where the time goes in v2:
time: 513 us; the launch traced here: 511 us
  Pallas kernels  509 us (99%)
    pallas_call x1, Pallas kernels, sweep(): pl.pallas_call(functools.partial(main_kernel, groups, peers, rows, cut),...  497 us
    pallas_call x1, Pallas kernels, close(): pl.pallas_call(close_kernel, out_shape=jax.ShapeDtypeStruct(image.shape,...  12.1 us

profile of v2, /device:TPU:0, one launch (start us, length us, event | category | flops | bytes accessed | tf_op | source)
XLA Modules:
  0.0 511.2 jit_solution(17740894265001824038)
XLA Ops:
  0.6 497.2 %shard_map.67 = (bf16[80,100,640]{2,1,0:T(8,128)(2,1)}, bf16[80,100,640]{2,1,0:T(8,128)(2,1)}, bf16[100,80,640]{2,1,0:T(8,128)(2,1)}, bf16[100,80,256]{2,1,0:T(8...) custom-call(bf16[640,640]{1,0:T(8,128)(2,1)} %fock_ref.1, ...), custom_call_target="tpu_custom_call" | custom-call | tf_op jit(solution)/shard_map/pallas_call | solution.py:634
  497.8 12.1 %shard_map.68 = bf16[100,80,640]{2,1,0:T(8,128)(2,1)} custom-call(f32[8,128]{1,0:T(8,128)} %get-tuple-element.6.stats_ref, bf16[100,80,640]{2,1,0:T(8,128)(2,1)} %get-tuple-element.7.apart_ref, bf16[100,80,640]{2,1,0:T(8,128)(2,1)} %get-tuple-element.8.image_ref), custom_call_target="tpu_custom_call" | custom-call | tf_op jit(solution)/shard_map/pallas_call | solution.py:721
  510.0 1.3 fusion
